TPU v7x, 256 devices: a 8x8x2 block of a 8x8x16 slice. The times are simulated.
256 devices in a mesh: groups: 2 (over z), seq: 128 (over x, y, core).
Axes of the slice: x: 8, y: 8, z: 2, core: 2. Of those that a mesh axis runs over, the one named last changes fastest.
The devices are a block of a 8x8x16 slice.
Arguments:
- query_rows: bfloat16 [131072, 1536], P(('groups', 'seq')), parts along dimension 0, may hold values from -200 to 200
- key_rows: bfloat16 [131072, 1536], P(('groups', 'seq')), parts along dimension 0, may hold values from -6 to 6
- value_rows: bfloat16 [131072, 1536], P(('groups', 'seq')), parts along dimension 0, may hold values from -6 to 6
- select: int32 [512, 6], P('groups'), parts along dimension 0, may hold values from 0 to 255, as said below
- counts: int32 [512], P('groups'), parts along dimension 0, may hold values from 2 to 6, as said below
- guide_scale: float32 [2], P('groups'), parts along dimension 0, may hold values from 4 to 8
Outputs:
- guided: bfloat16 [65536, 1536], P(('groups', 'seq')), parts along dimension 0
There are 2 independent parts, one for each index of `groups`. A program takes and returns all parts, laid end to end along the dimension named above; each array names one. Nothing has to cross between parts.
Inputs may be any that keep to these rules, and one draw needn't show every extreme that they name: Row i begins with i itself. Its first counts[i] entries are distinct and name tiles of shards within 2 of tile i's shard, where tile t belongs to shard t // 4. The query tiles of one shard select at most 2 distinct tiles of any one other shard, and every shard selects 2 tiles of each shard within 2 in every draw. Entries past counts[i] are valid tile numbers that are not used. `counts`: whole shards are heavy or light, so the work of one device differs by about two times between devices.
All inputs are finite; a program needn't handle non-finite values.
Results may differ from a plain program's by a relative error of at most 0.0075.
Values may be sent and summed in bfloat16 or wider, within the bound.
A program may use at most 128 MiB of HBM per device.

v0:
```python
import jax
import jax.numpy as jnp
from jax import lax
from jax.sharding import PartitionSpec as P

HEADS = 12
HEAD_DIM = 128
TILE = 128
REACH = 2
CAP = 2


def shifted(block, axis, distance):
    devices = range(lax.axis_size(axis))
    route = [(i - distance, i) for i in devices if i - distance in devices]
    return lax.ppermute(block, axis, route)


def partner(block, axis, stride):
    count = lax.axis_size(axis)
    route = []
    for low in range(count):
        high = low | 1 << stride
        if high != low and high < count:
            route += [(low, high), (high, low)]
    return lax.ppermute(block, axis, route)


def need_mask(select, counts, query_shard, owner_shard, shards, tiles_dev):
    usable = (
        (query_shard >= 0) & (query_shard < shards) & (owner_shard >= 0) & (owner_shard < shards)
    )
    first_row = jnp.clip(query_shard, 0, shards - 1) * tiles_dev
    chosen_rows = lax.dynamic_slice_in_dim(select, first_row, tiles_dev, 0)
    live_counts = lax.dynamic_slice_in_dim(counts, first_row, tiles_dev, 0)
    alive_slots = jnp.arange(select.shape[1], dtype=jnp.int32)[None, :] < live_counts[:, None]
    owned_tiles = owner_shard * tiles_dev + jnp.arange(tiles_dev, dtype=jnp.int32)
    matches = (chosen_rows[:, :, None] == owned_tiles[None, None, :]) & alive_slots[:, :, None]
    wanted_any = jnp.any(matches, axis=(0, 1)) & usable
    ranking = jnp.cumsum(wanted_any.astype(jnp.int32)) - 1
    return (wanted_any, ranking)


def body(query_rows, key_rows, value_rows, select, counts, guide_scale):
    devices_seq = lax.axis_size("seq")
    shards = devices_seq // 2
    my_index = lax.axis_index("seq")
    my_shard = my_index // 2
    my_half = my_index % 2
    tokens, row_width = query_rows.shape
    tiles_dev = tokens // TILE
    pick_count = select.shape[1]
    offsets = [shift_by for shift_by in range(-REACH, REACH + 1) if shift_by != 0]
    flat_keys = key_rows.reshape(tiles_dev, TILE * row_width)
    flat_values = value_rows.reshape(tiles_dev, TILE * row_width)
    received = []
    rankings = []
    per_owner = CAP
    slot_ids = jnp.arange(CAP, dtype=jnp.int32)
    for shift_by in offsets:
        wanted_out, rank_out = need_mask(
            select, counts, my_shard + shift_by, my_shard, shards, tiles_dev
        )
        chooser = ((rank_out[None, :] == slot_ids[:, None]) & wanted_out[None, :]).astype(
            jnp.bfloat16
        )
        send_keys = jnp.dot(chooser, flat_keys, preferred_element_type=jnp.float32).astype(
            jnp.bfloat16
        )
        send_values = jnp.dot(chooser, flat_values, preferred_element_type=jnp.float32).astype(
            jnp.bfloat16
        )
        received.append(shifted((send_keys, send_values), "seq", 2 * shift_by))
        wanted_in, rank_in = need_mask(
            select, counts, my_shard, my_shard - shift_by, shards, tiles_dev
        )
        rankings.append(rank_in)
    pool_keys = jnp.concatenate([flat_keys] + [landed[0] for landed in received], axis=0)
    pool_values = jnp.concatenate([flat_values] + [landed[1] for landed in received], axis=0)
    my_first = my_shard * tiles_dev
    my_select = lax.dynamic_slice_in_dim(select, my_first, tiles_dev, 0)
    my_counts = lax.dynamic_slice_in_dim(counts, my_first, tiles_dev, 0)
    owners = my_select // tiles_dev
    within = my_select % tiles_dev
    distance = my_shard - owners
    position = jnp.clip(
        jnp.where(distance < 0, distance + REACH, distance + REACH - 1), 0, 2 * REACH - 1
    )
    rank_table = jnp.stack(rankings).reshape(-1)
    flat_slot = position * tiles_dev + within
    table_ids = jnp.arange(rank_table.shape[0], dtype=jnp.int32)
    rank_pick = jnp.sum(
        jnp.where(flat_slot[:, :, None] == table_ids[None, None, :], rank_table[None, None, :], 0),
        axis=2,
    )
    pool_slot = jnp.where(owners == my_shard, within, tiles_dev + position * per_owner + rank_pick)
    pool_slot = jnp.clip(pool_slot, 0, pool_keys.shape[0] - 1)
    alive_slots = jnp.arange(pick_count, dtype=jnp.int32)[None, :] < my_counts[:, None]
    query_heads = query_rows.reshape(tiles_dev, TILE, HEADS, HEAD_DIM)
    score_scale = HEAD_DIM ** (-0.5)

    def attend(pick_index, running):
        row_max, denominator, weighted = running
        slot_now = lax.dynamic_index_in_dim(pool_slot, pick_index, 1, keepdims=False)
        alive_now = lax.dynamic_index_in_dim(alive_slots, pick_index, 1, keepdims=False)
        key_tile = pool_keys[slot_now].reshape(tiles_dev, TILE, HEADS, HEAD_DIM)
        value_tile = pool_values[slot_now].reshape(tiles_dev, TILE, HEADS, HEAD_DIM)
        scores = (
            jnp.einsum("athd,ashd->aths", query_heads, key_tile, preferred_element_type=jnp.float32)
            * score_scale
        )
        scores = jnp.where(alive_now[:, None, None, None], scores, -jnp.inf)
        new_max = jnp.maximum(row_max, jnp.max(scores, axis=3))
        decay_factor = jnp.exp(row_max - new_max)
        weights = jnp.exp(scores - new_max[..., None])
        denominator = denominator * decay_factor + jnp.sum(weights, axis=3)
        update = jnp.einsum(
            "aths,ashd->athd",
            weights.astype(jnp.bfloat16),
            value_tile,
            preferred_element_type=jnp.float32,
        )
        weighted = weighted * decay_factor[..., None] + update
        return (new_max, denominator, weighted)

    starting = (
        jnp.full((tiles_dev, TILE, HEADS), -jnp.inf, jnp.float32),
        jnp.zeros((tiles_dev, TILE, HEADS), jnp.float32),
        jnp.zeros((tiles_dev, TILE, HEADS, HEAD_DIM), jnp.float32),
    )
    last_pick = jnp.max(my_counts)
    finished = lax.fori_loop(0, last_pick, attend, starting)
    branch_out = (
        (finished[2] / finished[1][..., None]).reshape(tokens, row_width).astype(jnp.bfloat16)
    )
    guidance = guide_scale[0]
    half_rows = tokens // 2
    kept_rows = lax.dynamic_slice_in_dim(branch_out, my_half * half_rows, half_rows, 0)
    sent_rows = lax.dynamic_slice_in_dim(branch_out, (1 - my_half) * half_rows, half_rows, 0)
    from_partner = partner(sent_rows, "seq", 0)
    own_rows = lax.optimization_barrier(kept_rows).astype(jnp.float32)
    theirs = from_partner.astype(jnp.float32)
    cond_out = jnp.where(my_half == 0, own_rows, theirs)
    uncond = jnp.where(my_half == 0, theirs, own_rows)
    result = uncond + guidance * (cond_out - uncond)
    return result.astype(jnp.bfloat16)


def solution(mesh):
    in_specs = (
        P(("groups", "seq"), None),
        P(("groups", "seq"), None),
        P(("groups", "seq"), None),
        P("groups", None),
        P("groups"),
        P("groups"),
    )
    out_specs = P(("groups", "seq"), None)
    return jax.shard_map(body, mesh=mesh, in_specs=in_specs, out_specs=out_specs, check_vma=False)
```

profile of v0, /device:TPU:549, one launch (start us, length us, event | category | flops | bytes accessed | tf_op | source)
XLA Modules:
  0.0 514.0 jit_solution(1724479581396796000)
XLA Ops:
  18.6 6.9 %collective-permute-start.7 = (bf16[2,196608]{1,0:T(2,128)(2,1)}, bf16[2,196608]{1,0:T(2,128)(2,1)}, u32[]{:S(2)}, u32[]{:S(2)}) collective-permute-start(bf16[2,196608]{1,0:T(2,128)(2,1)} %convolution_convert_fusion), channel_id=1, source_target_pairs={{0,4},{1,5},{2,6},{3,7},{4,8},{5,9},{6,10},{7,11},{8,12},{9,13},{1... | collective-permute-start | bytes 2359304 | tf_op jit(solution)/shard_map/ppermute | solution.py:16
  51.9 6.2 %collective-permute-done.7 = bf16[2,196608]{1,0:T(2,128)(2,1)} collective-permute-done((bf16[2,196608]{1,0:T(2,128)(2,1)}, bf16[2,196608]{1,0:T(2,128)(2,1)}, u32[]{:S(2)}, u32[]{:S(2)}) %collective-permute-start.7) | collective-permute-done | bytes 786464 | tf_op jit(solution)/shard_map/ppermute | solution.py:16
  58.1 7.2 %collective-permute-start = (bf16[2,196608]{1,0:T(2,128)(2,1)}, bf16[2,196608]{1,0:T(2,128)(2,1)}, u32[]{:S(2)}, u32[]{:S(2)}) collective-permute-start(bf16[2,196608]{1,0:T(2,128)(2,1)} %convolution_convert_fusion.7), channel_id=1, source_target_pairs={{4,0},{5,1},{6,2},{7,3},{8,4},{9,5},{10,6},{11,7},{12,8},{13,9},{1... | collective-permute-start | bytes 2359304 | tf_op jit(solution)/shard_map/ppermute | solution.py:16
  70.4 27.4 %concatenate.7 = bf16[12,196608]{1,0:T(8,128)(2,1)} concatenate(bf16[4,196608]{1,0:T(4,128)(2,1)} %copy-done.2, bf16[2,196608]{1,0:T(2,128)(2,1)} %collective-permute-done.4, bf16[2,196608]{1,0:T(2,128)(2,1)} %collective-permute-done.5, bf16[2,196608]{1,0:T(2,128)(2,1)} %collective-permute-done.6, bf16[2,196608]{1,0:T(2,128)(2,1)} %collective-permute-done.7), dimensions={0} | concatenate | bytes 9437184 | tf_op jit(solution)/shard_map/concatenate | solution.py:79
  97.8 19.6 %collective-permute-done.2 = bf16[2,196608]{1,0:T(2,128)(2,1)} collective-permute-done((bf16[2,196608]{1,0:T(2,128)(2,1)}, bf16[2,196608]{1,0:T(2,128)(2,1)}, u32[]{:S(2)}, u32[]{:S(2)}) %collective-permute-start.2) | collective-permute-done | bytes 786464 | tf_op jit(solution)/shard_map/ppermute | solution.py:16
  117.4 26.4 %concatenate.6 = bf16[12,196608]{1,0:T(8,128)(2,1)} concatenate(bf16[4,196608]{1,0:T(4,128)(2,1)S(1)} %copy-done.4, bf16[2,196608]{1,0:T(2,128)(2,1)} %collective-permute-done, bf16[2,196608]{1,0:T(2,128)(2,1)} %collective-permute-done.1, bf16[2,196608]{1,0:T(2,128)(2,1)} %collective-permute-done.2, bf16[2,196608]{1,0:T(2,128)(2,1)S(1)} %collective-permute-done.3), dimensions={0} | concatenate | bytes 9437184 | tf_op jit(solution)/shard_map/concatenate | solution.py:78
  145.9 330.1 %while.14 = (s32[]{:T(128)}, f32[4,128,12]{1,2,0:T(8,128)S(1)}, f32[4,128,12]{1,2,0:T(8,128)S(1)}, f32[4,128,12,128]{1,3,2,0:T(8,128)}, s32[]{:T(128)}, /*index=...) while((s32[]{:T(128)}, f32[4,128,12]{1,2,0:T(8,128)S(1)}, ...), condition=%wide.region_21.22_spmd, body=%wide.region_18.21_spmd.sunk | while | flops 419181568 | bytes 83759456 | solution.py:132
  146.5 8.6 %fusion.61 = (bf16[12,98304]{1,0:T(8,128)(2,1)S(1)}, bf16[12,98304]{1,0:T(8,128)(2,1)}, bf16[12,98304]{1,0:T(8,128)(2,1)}, bf16[12,98304]{1,0:T(8,128)(2,1)}) fusion(bf16[12,196608]{1,0:T(8,128)(2,1)} %get-tuple-element.265, bf16[12,196608]{1,0:T(8,128)(2,1)} %get-tuple-element.263), kind=kLoop, calls=%fused_computation.128.clone.1 | loop fusion | bytes 18874368 | tf_op jit(solution)/shard_map/while/body/gather | solution.py:107
  160.2 5.1 gather_fusion.1
  179.1 5.1 gather_fusion.2
  195.3 5.4 %bitcast_add_fusion.2 = f32[4,128,12,128]{1,3,2,0:T(8,128)} fusion(f32[4,128,12,128]{1,3,2,0:T(8,128)} %get-tuple-element.246, f32[4,12,128,128]{3,2,1,0:T(8,128)S(1)} %copy-done.1, bf16[4,128,12,128]{3,2,1,0:T(8,128)(2,1)} %reshape.478, f32[4,128,12]{1,2,0:T(8,128)S(1)} %get-tuple-element.229, f32[4,128,12]{1,2,0:T(8,128)S(1)} %max.39, ...), kind=kOutput, calls=%fused_computation.4.clone.1 | convolution fusion | flops 206045184 | bytes 11059204 | tf_op jit(solution)/shard_map/while/body/aths,ashd->athd/dot_general | solution.py:117
  201.4 8.6 %fusion.61 = (bf16[12,98304]{1,0:T(8,128)(2,1)S(1)}, bf16[12,98304]{1,0:T(8,128)(2,1)}, bf16[12,98304]{1,0:T(8,128)(2,1)}, bf16[12,98304]{1,0:T(8,128)(2,1)}) fusion(bf16[12,196608]{1,0:T(8,128)(2,1)} %get-tuple-element.265, bf16[12,196608]{1,0:T(8,128)(2,1)} %get-tuple-element.263), kind=kLoop, calls=%fused_computation.128.clone.1 | loop fusion | bytes 18874368 | tf_op jit(solution)/shard_map/while/body/gather | solution.py:107
  215.1 5.1 gather_fusion.1
  234.0 5.1 gather_fusion.2
  250.2 5.4 %bitcast_add_fusion.2 = f32[4,128,12,128]{1,3,2,0:T(8,128)} fusion(f32[4,128,12,128]{1,3,2,0:T(8,128)} %get-tuple-element.246, f32[4,12,128,128]{3,2,1,0:T(8,128)S(1)} %copy-done.1, bf16[4,128,12,128]{3,2,1,0:T(8,128)(2,1)} %reshape.478, f32[4,128,12]{1,2,0:T(8,128)S(1)} %get-tuple-element.229, f32[4,128,12]{1,2,0:T(8,128)S(1)} %max.39, ...), kind=kOutput, calls=%fused_computation.4.clone.1 | convolution fusion | flops 206045184 | bytes 11059204 | tf_op jit(solution)/shard_map/while/body/aths,ashd->athd/dot_general | solution.py:117
  256.3 8.6 %fusion.61 = (bf16[12,98304]{1,0:T(8,128)(2,1)S(1)}, bf16[12,98304]{1,0:T(8,128)(2,1)}, bf16[12,98304]{1,0:T(8,128)(2,1)}, bf16[12,98304]{1,0:T(8,128)(2,1)}) fusion(bf16[12,196608]{1,0:T(8,128)(2,1)} %get-tuple-element.265, bf16[12,196608]{1,0:T(8,128)(2,1)} %get-tuple-element.263), kind=kLoop, calls=%fused_computation.128.clone.1 | loop fusion | bytes 18874368 | tf_op jit(solution)/shard_map/while/body/gather | solution.py:107
  270.0 5.1 gather_fusion.1
  288.8 5.1 gather_fusion.2
  305.1 5.4 %bitcast_add_fusion.2 = f32[4,128,12,128]{1,3,2,0:T(8,128)} fusion(f32[4,128,12,128]{1,3,2,0:T(8,128)} %get-tuple-element.246, f32[4,12,128,128]{3,2,1,0:T(8,128)S(1)} %copy-done.1, bf16[4,128,12,128]{3,2,1,0:T(8,128)(2,1)} %reshape.478, f32[4,128,12]{1,2,0:T(8,128)S(1)} %get-tuple-element.229, f32[4,128,12]{1,2,0:T(8,128)S(1)} %max.39, ...), kind=kOutput, calls=%fused_computation.4.clone.1 | convolution fusion | flops 206045184 | bytes 11059204 | tf_op jit(solution)/shard_map/while/body/aths,ashd->athd/dot_general | solution.py:117
  311.2 8.6 %fusion.61 = (bf16[12,98304]{1,0:T(8,128)(2,1)S(1)}, bf16[12,98304]{1,0:T(8,128)(2,1)}, bf16[12,98304]{1,0:T(8,128)(2,1)}, bf16[12,98304]{1,0:T(8,128)(2,1)}) fusion(bf16[12,196608]{1,0:T(8,128)(2,1)} %get-tuple-element.265, bf16[12,196608]{1,0:T(8,128)(2,1)} %get-tuple-element.263), kind=kLoop, calls=%fused_computation.128.clone.1 | loop fusion | bytes 18874368 | tf_op jit(solution)/shard_map/while/body/gather | solution.py:107
  324.9 5.1 gather_fusion.1
  343.7 5.1 gather_fusion.2
  360.0 5.4 %bitcast_add_fusion.2 = f32[4,128,12,128]{1,3,2,0:T(8,128)} fusion(f32[4,128,12,128]{1,3,2,0:T(8,128)} %get-tuple-element.246, f32[4,12,128,128]{3,2,1,0:T(8,128)S(1)} %copy-done.1, bf16[4,128,12,128]{3,2,1,0:T(8,128)(2,1)} %reshape.478, f32[4,128,12]{1,2,0:T(8,128)S(1)} %get-tuple-element.229, f32[4,128,12]{1,2,0:T(8,128)S(1)} %max.39, ...), kind=kOutput, calls=%fused_computation.4.clone.1 | convolution fusion | flops 206045184 | bytes 11059204 | tf_op jit(solution)/shard_map/while/body/aths,ashd->athd/dot_general | solution.py:117
  366.0 8.6 %fusion.61 = (bf16[12,98304]{1,0:T(8,128)(2,1)S(1)}, bf16[12,98304]{1,0:T(8,128)(2,1)}, bf16[12,98304]{1,0:T(8,128)(2,1)}, bf16[12,98304]{1,0:T(8,128)(2,1)}) fusion(bf16[12,196608]{1,0:T(8,128)(2,1)} %get-tuple-element.265, bf16[12,196608]{1,0:T(8,128)(2,1)} %get-tuple-element.263), kind=kLoop, calls=%fused_computation.128.clone.1 | loop fusion | bytes 18874368 | tf_op jit(solution)/shard_map/while/body/gather | solution.py:107
  379.8 5.1 gather_fusion.1
  398.6 5.1 gather_fusion.2
  414.9 5.4 %bitcast_add_fusion.2 = f32[4,128,12,128]{1,3,2,0:T(8,128)} fusion(f32[4,128,12,128]{1,3,2,0:T(8,128)} %get-tuple-element.246, f32[4,12,128,128]{3,2,1,0:T(8,128)S(1)} %copy-done.1, bf16[4,128,12,128]{3,2,1,0:T(8,128)(2,1)} %reshape.478, f32[4,128,12]{1,2,0:T(8,128)S(1)} %get-tuple-element.229, f32[4,128,12]{1,2,0:T(8,128)S(1)} %max.39, ...), kind=kOutput, calls=%fused_computation.4.clone.1 | convolution fusion | flops 206045184 | bytes 11059204 | tf_op jit(solution)/shard_map/while/body/aths,ashd->athd/dot_general | solution.py:117
  420.9 8.6 %fusion.61 = (bf16[12,98304]{1,0:T(8,128)(2,1)S(1)}, bf16[12,98304]{1,0:T(8,128)(2,1)}, bf16[12,98304]{1,0:T(8,128)(2,1)}, bf16[12,98304]{1,0:T(8,128)(2,1)}) fusion(bf16[12,196608]{1,0:T(8,128)(2,1)} %get-tuple-element.265, bf16[12,196608]{1,0:T(8,128)(2,1)} %get-tuple-element.263), kind=kLoop, calls=%fused_computation.128.clone.1 | loop fusion | bytes 18874368 | tf_op jit(solution)/shard_map/while/body/gather | solution.py:107
  434.6 5.1 gather_fusion.1
  453.5 5.1 gather_fusion.2
  469.8 5.4 %bitcast_add_fusion.2 = f32[4,128,12,128]{1,3,2,0:T(8,128)} fusion(f32[4,128,12,128]{1,3,2,0:T(8,128)} %get-tuple-element.246, f32[4,12,128,128]{3,2,1,0:T(8,128)S(1)} %copy-done.1, bf16[4,128,12,128]{3,2,1,0:T(8,128)(2,1)} %reshape.478, f32[4,128,12]{1,2,0:T(8,128)S(1)} %get-tuple-element.229, f32[4,128,12]{1,2,0:T(8,128)S(1)} %max.39, ...), kind=kOutput, calls=%fused_computation.4.clone.1 | convolution fusion | flops 206045184 | bytes 11059204 | tf_op jit(solution)/shard_map/while/body/aths,ashd->athd/dot_general | solution.py:117
  480.0 30.5 %collective-permute-start.8 = (bf16[256,1536]{0,1:T(8,128)(2,1)S(1)}, bf16[256,1536]{0,1:T(8,128)(2,1)S(1)}, u32[]{:S(2)}, u32[]{:S(2)}) collective-permute-start(bf16[256,1536]{0,1:T(8,128)(2,1)S(1)} %get-tuple-element.129), channel_id=1, source_target_pairs={{0,1},{1,0},{2,3},{3,2},{4,5},{5,4},{6,7},{7,6},{8,9},{9,8},{10,11... | collective-permute-start | bytes 2359304 | tf_op jit(solution)/shard_map/ppermute | solution.py:26
  (196 shorter events, 238.8 us)
Async XLA Ops:
  6.2 19.6 %copy-start.2 = (bf16[4,196608]{1,0:T(4,128)(2,1)}, bf16[4,196608]{1,0:T(4,128)(2,1)S(1)}, u32[]{:S(2)}) copy-start(bf16[4,196608]{1,0:T(4,128)(2,1)S(1)} %reshape.417) | copy-start | bytes 4718596
  8.1 37.0 %collective-permute-start.5 = (bf16[2,196608]{1,0:T(2,128)(2,1)}, bf16[2,196608]{1,0:T(2,128)(2,1)}, u32[]{:S(2)}, u32[]{:S(2)}) collective-permute-start(bf16[2,196608]{1,0:T(2,128)(2,1)} %convolution_convert_fusion.2), channel_id=1, source_target_pairs={{2,0},{3,1},{4,2},{5,3},{6,4},{7,5},{8,6},{9,7},{10,8},{11,9},{12,... | collective-permute-start | bytes 2359304 | tf_op jit(solution)/shard_map/ppermute | solution.py:16
  12.1 37.9 %collective-permute-start.6 = (bf16[2,196608]{1,0:T(2,128)(2,1)}, bf16[2,196608]{1,0:T(2,128)(2,1)}, u32[]{:S(2)}, u32[]{:S(2)}) collective-permute-start(bf16[2,196608]{1,0:T(2,128)(2,1)} %convolution_convert_fusion.1), channel_id=1, source_target_pairs={{0,2},{1,3},{2,4},{3,5},{4,6},{5,7},{6,8},{7,9},{8,10},{9,11},{10,... | collective-permute-start | bytes 2359304 | tf_op jit(solution)/shard_map/ppermute | solution.py:16
  18.6 39.5 %collective-permute-start.7 = (bf16[2,196608]{1,0:T(2,128)(2,1)}, bf16[2,196608]{1,0:T(2,128)(2,1)}, u32[]{:S(2)}, u32[]{:S(2)}) collective-permute-start(bf16[2,196608]{1,0:T(2,128)(2,1)} %convolution_convert_fusion), channel_id=1, source_target_pairs={{0,4},{1,5},{2,6},{3,7},{4,8},{5,9},{6,10},{7,11},{8,12},{9,13},{1... | collective-permute-start | bytes 2359304 | tf_op jit(solution)/shard_map/ppermute | solution.py:16
  25.8 5.4 %copy-start.5 = (bf16[512,1536]{1,0:T(8,128)(2,1)S(1)}, bf16[512,1536]{1,0:T(8,128)(2,1)}, u32[]{:S(2)}) copy-start(bf16[512,1536]{1,0:T(8,128)(2,1)} %param.9) | copy-start | bytes 4718596
  27.6 42.7 %collective-permute-start.4 = (bf16[2,196608]{1,0:T(2,128)(2,1)}, bf16[2,196608]{1,0:T(2,128)(2,1)}, u32[]{:S(2)}, u32[]{:S(2)}) collective-permute-start(bf16[2,196608]{1,0:T(2,128)(2,1)} %convolution_convert_fusion.3), channel_id=1, source_target_pairs={{4,0},{5,1},{6,2},{7,3},{8,4},{9,5},{10,6},{11,7},{12,8},{13,9},{1... | collective-permute-start | bytes 2359304 | tf_op jit(solution)/shard_map/ppermute | solution.py:16
  32.4 10.9 %copy-start.3 = (bf16[4,196608]{1,0:T(4,128)(2,1)}, bf16[4,196608]{1,0:T(4,128)(2,1)S(1)}, u32[]{:S(2)}) copy-start(bf16[4,196608]{1,0:T(4,128)(2,1)S(1)} %reshape.415) | copy-start | bytes 4718596
  34.2 63.6 %collective-permute-start.3 = (bf16[2,196608]{1,0:T(2,128)(2,1)}, bf16[2,196608]{1,0:T(2,128)(2,1)S(1)}, u32[]{:S(2)}, u32[]{:S(2)}) collective-permute-start(bf16[2,196608]{1,0:T(2,128)(2,1)} %convolution_convert_fusion.4), channel_id=1, source_target_pairs={{0,4},{1,5},{2,6},{3,7},{4,8},{5,9},{6,10},{7,11},{8,12},{9,13},{1... | collective-permute-start | bytes 2359304 | tf_op jit(solution)/shard_map/ppermute | solution.py:16
  45.1 72.3 %collective-permute-start.2 = (bf16[2,196608]{1,0:T(2,128)(2,1)}, bf16[2,196608]{1,0:T(2,128)(2,1)}, u32[]{:S(2)}, u32[]{:S(2)}) collective-permute-start(bf16[2,196608]{1,0:T(2,128)(2,1)} %convolution_convert_fusion.5), channel_id=1, source_target_pairs={{0,2},{1,3},{2,4},{3,5},{4,6},{5,7},{6,8},{7,9},{8,10},{9,11},{10,... | collective-permute-start | bytes 2359304 | tf_op jit(solution)/shard_map/ppermute | solution.py:16
  50.0 67.5 %collective-permute-start.1 = (bf16[2,196608]{1,0:T(2,128)(2,1)}, bf16[2,196608]{1,0:T(2,128)(2,1)}, u32[]{:S(2)}, u32[]{:S(2)}) collective-permute-start(bf16[2,196608]{1,0:T(2,128)(2,1)} %convolution_convert_fusion.6), channel_id=1, source_target_pairs={{2,0},{3,1},{4,2},{5,3},{6,4},{7,5},{8,6},{9,7},{10,8},{11,9},{12,... | collective-permute-start | bytes 2359304 | tf_op jit(solution)/shard_map/ppermute | solution.py:16
  58.1 59.3 %collective-permute-start = (bf16[2,196608]{1,0:T(2,128)(2,1)}, bf16[2,196608]{1,0:T(2,128)(2,1)}, u32[]{:S(2)}, u32[]{:S(2)}) collective-permute-start(bf16[2,196608]{1,0:T(2,128)(2,1)} %convolution_convert_fusion.7), channel_id=1, source_target_pairs={{4,0},{5,1},{6,2},{7,3},{8,4},{9,5},{10,6},{11,7},{12,8},{13,9},{1... | collective-permute-start | bytes 2359304 | tf_op jit(solution)/shard_map/ppermute | solution.py:16
  68.3 1.9 copy-start.6
  70.3 47.1 %copy-start.4 = (bf16[4,196608]{1,0:T(4,128)(2,1)S(1)}, bf16[4,196608]{1,0:T(4,128)(2,1)}, u32[]{:S(2)}) copy-start(bf16[4,196608]{1,0:T(4,128)(2,1)} %copy-done.3) | copy-start | bytes 4718596
  177.4 1.7 copy-start
  190.8 4.5 copy-start.1
  232.3 1.7 copy-start
  245.7 4.5 copy-start.1
  287.2 1.7 copy-start
  300.6 4.5 copy-start.1
  342.0 1.7 copy-start
  355.5 4.5 copy-start.1
  396.9 1.7 copy-start
  410.3 4.5 copy-start.1
  451.8 1.7 copy-start
  465.2 4.5 copy-start.1
  480.0 32.4 %collective-permute-start.8 = (bf16[256,1536]{0,1:T(8,128)(2,1)S(1)}, bf16[256,1536]{0,1:T(8,128)(2,1)S(1)}, u32[]{:S(2)}, u32[]{:S(2)}) collective-permute-start(bf16[256,1536]{0,1:T(8,128)(2,1)S(1)} %get-tuple-element.129), channel_id=1, source_target_pairs={{0,1},{1,0},{2,3},{3,2},{4,5},{5,4},{6,7},{7,6},{8,9},{9,8},{10,11... | collective-permute-start | bytes 2359304 | tf_op jit(solution)/shard_map/ppermute | solution.py:26
where the time goes:
time: 522 us; the launch traced here: 514 us
  local copies, waits for them, and re-layouts  282 us (54%)
  other arithmetic  67.3 us (13%)
  matrix products  66.8 us (13%)
  starting transfers between devices  65.4 us (13%)
  waiting for transfers between devices  27.1 us (5%)
    gather x18, local copies, waits for them, and re-layouts, attend(): value_tile = pool_values[slot_now].reshape(tiles_dev, TILE, HEADS, HEAD_DIM)  95.2 us
    gather x12, local copies, waits for them, and re-layouts, attend(): key_tile = pool_keys[slot_now].reshape(tiles_dev, TILE, HEADS, HEAD_DIM)  60.9 us
    while x12, other arithmetic  53.9 us
    ppermute x8, starting transfers between devices, shifted(): return lax.ppermute(block, axis, route)  34.9 us
    dot_general x6, matrix products, attend(): jnp.einsum('aths,ashd->athd', weights.astype(jnp.bfloat16), value_tile, p...  32.5 us
    ppermute x1, starting transfers between devices, partner(): return lax.ppermute(block, axis, route)  30.5 us
    concatenate x1, local copies, waits for them, and re-layouts, body(): jnp.concatenate([flat_values] + [landed[1] for landed in received], axis=0)  27.4 us
    reshape x6, local copies, waits for them, and re-layouts, attend(): value_tile = pool_values[slot_now].reshape(tiles_dev, TILE, HEADS, HEAD_DIM)  27.3 us
  transfers between devices with their start and end apart: 9, of which 3 were waited for; matrix products, arithmetic and copies ran while one was open for 9% of the time, Pallas kernels for 0%

commit v1 on v0

v1 whole, which is shorter than its diff:
```python
import jax
import jax.numpy as jnp
from jax import lax
from jax.experimental import pallas as pl
from jax.experimental.pallas import tpu as pltpu
from jax.sharding import PartitionSpec as P

HEAD_DIM = 128
TILE = 128
REACH = 2
CAP = 2
OFFSETS = (-2, 2, -1, 1)
AHEAD = 3
LOG2E = 1.4426950408889634
MESH = pl.DeviceIdType.MESH


def lowest_bit(bits):
    return bits & -bits


def kernel(
    query_hbm,
    key_hbm,
    value_hbm,
    select,
    counts,
    guide_scale,
    out_hbm,
    queries,
    own,
    staged,
    pool,
    branch_out,
    theirs,
    mixed,
    bias,
    send_bits,
    load_sem,
    send_sem,
    recv_sem,
    swap_send_sem,
    swap_recv_sem,
    out_sem,
):
    heads, tokens, _ = queries.shape
    tiles_dev = tokens // TILE
    half_rows = tokens // 2
    picks = select.shape[0]
    devices = lax.axis_size("seq")
    shards = devices // 2
    me = lax.axis_index("seq")
    shard = me // 2
    half = me % 2
    partner = me + 1 - 2 * half
    places = range(len(OFFSETS))

    def inside(place, sign):
        other = shard + sign * OFFSETS[place]
        return (other >= 0) & (other < shards)

    def columns(head):
        return pl.ds(pl.multiple_of(head * HEAD_DIM, HEAD_DIM), HEAD_DIM)

    def load(head, which):
        source = (key_hbm, value_hbm, query_hbm)[which]
        target = queries.at[head] if which == 2 else own.at[head, which]
        return pltpu.make_async_copy(
            source.at[:, columns(head)], target, load_sem.at[head, which]
        )

    def send(head, place):
        target = jnp.clip(me + 2 * OFFSETS[place], 0, devices - 1)
        return pltpu.make_async_remote_copy(
            src_ref=staged.at[head, place],
            dst_ref=pool.at[head, place],
            send_sem=send_sem.at[head, place],
            recv_sem=recv_sem.at[head, place],
            device_id={"seq": target},
            device_id_type=MESH,
        )

    def swap(head):
        return pltpu.make_async_remote_copy(
            src_ref=branch_out.at[head, pl.ds((1 - half) * half_rows, half_rows)],
            dst_ref=theirs.at[head],
            send_sem=swap_send_sem.at[head],
            recv_sem=swap_recv_sem.at[head],
            device_id={"seq": partner},
            device_id_type=MESH,
        )

    def write(head):
        return pltpu.make_async_copy(
            mixed.at[head], out_hbm.at[:, columns(head)], out_sem.at[head]
        )

    def start_loads(head, carry):
        for which in range(3):
            load(head, which).start()
        return carry

    lax.fori_loop(0, heads, start_loads, 0)

    barrier = pltpu.get_barrier_semaphore()
    pl.semaphore_signal(barrier, inc=1, device_id={"seq": partner}, device_id_type=MESH)
    greeted = jnp.int32(1)
    for place in places:
        there = inside(place, 1)
        greeted += there.astype(jnp.int32)

        @pl.when(there)
        def _():
            pl.semaphore_signal(
                barrier,
                inc=1,
                device_id={"seq": me + 2 * OFFSETS[place]},
                device_id_type=MESH,
            )

    for place in places:
        asker = jnp.clip(shard + OFFSETS[place], 0, shards - 1)
        bits = jnp.int32(0)
        for row in range(tiles_dev):
            live = counts[asker * tiles_dev + row]
            for pick in range(picks):
                tile = select[pick, asker * tiles_dev + row] - shard * tiles_dev
                wanted = (pick < live) & (tile >= 0) & (tile < tiles_dev)
                bits |= jnp.where(wanted, 1 << (tile & (tiles_dev - 1)), 0)
        first = lowest_bit(bits)
        send_bits[2 * place] = first
        send_bits[2 * place + 1] = lowest_bit(bits ^ first)

    first_tile = (shard - REACH) * tiles_dev
    row_bits = []
    for row in range(tiles_dev):
        live = counts[shard * tiles_dev + row]
        bits = jnp.int32(0)
        for pick in range(picks):
            tile = select[pick, shard * tiles_dev + row] - first_tile
            bits |= jnp.where(pick < live, 1 << (tile & 31), 0)
        row_bits.append(bits)
    union = row_bits[0]
    for bits in row_bits[1:]:
        union |= bits
    pool_bits = [1 << (REACH * tiles_dev + tile) for tile in range(tiles_dev)]
    for place in places:
        base = (REACH - OFFSETS[place]) * tiles_dev
        block = union & (((1 << tiles_dev) - 1) << base)
        first = lowest_bit(block)
        pool_bits += [first, lowest_bit(block ^ first)]
    pool_tiles = len(pool_bits)
    for row in range(tiles_dev):
        for slot, bit in enumerate(pool_bits):
            bias[row * pool_tiles + slot] = jnp.where(
                (row_bits[row] & bit) != 0, jnp.float32(0), jnp.float32(-jnp.inf)
            )

    for place in places:

        @pl.when(jnp.logical_not(inside(place, -1)))
        def _():
            def clear(head, carry):
                pool[head, place] = jnp.zeros(pool.shape[2:], pool.dtype)
                return carry

            lax.fori_loop(0, heads, clear, 0)

    def stage(head):
        for which in range(2):
            load(head, which).wait()
        for which in range(2):
            tiles = [own[head, which, tile * TILE : (tile + 1) * TILE] for tile in range(tiles_dev)]
            for place in places:
                for slot in range(CAP):
                    bit = send_bits[2 * place + slot]
                    chosen = tiles[-1]
                    for tile in range(tiles_dev - 1):
                        chosen = jnp.where(bit == 1 << tile, tiles[tile], chosen)
                    row = (which * CAP + slot) * TILE
                    staged[head, place, row : row + TILE] = chosen

    def start_sends(head):
        for place in places:

            @pl.when(inside(place, 1))
            def _():
                send(head, place).start()

    stage(0)
    pl.semaphore_wait(barrier, greeted)

    def fill(head, carry):
        stage(head)

        @pl.when(head <= AHEAD)
        def _():
            start_sends(head - 1)

        return carry

    lax.fori_loop(1, heads, fill, 0)

    factor = HEAD_DIM ** (-0.5) * LOG2E
    across = (((1,), (1,)), ((), ()))

    def attend(head, side):
        rows = pl.multiple_of(side * half_rows, half_rows)
        query = queries[head, pl.ds(rows, half_rows)]
        raw = [lax.dot_general(query, own[head, 0], across, preferred_element_type=jnp.float32)]
        for place in places:
            raw.append(
                lax.dot_general(
                    query,
                    pool[head, place, : CAP * TILE],
                    across,
                    preferred_element_type=jnp.float32,
                )
            )
        blocks = []
        for block in raw:
            blocks += [block[:, at : at + TILE] for at in range(0, block.shape[1], TILE)]
        parts = []
        for part in range(half_rows // TILE):
            row = side * (half_rows // TILE) + part
            scores = [
                block[part * TILE : (part + 1) * TILE] + bias[row * pool_tiles + slot]
                for slot, block in enumerate(blocks)
            ]
            peak = scores[0]
            for score in scores[1:]:
                peak = jnp.maximum(peak, score)
            peak = jnp.max(peak, axis=1, keepdims=True)
            weights = [jnp.exp2((score - peak) * factor) for score in scores]
            total = weights[0]
            for weight in weights[1:]:
                total = total + weight
            total = jnp.sum(total, axis=1, keepdims=True)
            weights = [weight.astype(jnp.bfloat16) for weight in weights]
            parts.append((weights, total))
        stacked = [
            jnp.concatenate([weights[slot] for weights, _ in parts], axis=0)
            for slot in range(pool_tiles)
        ]
        totals = jnp.concatenate([total for _, total in parts], axis=0)
        update = jnp.dot(
            jnp.concatenate(stacked[:tiles_dev], axis=1),
            own[head, 1],
            preferred_element_type=jnp.float32,
        )
        for place in places:
            at = tiles_dev + CAP * place
            update += jnp.dot(
                jnp.concatenate(stacked[at : at + CAP], axis=1),
                pool[head, place, CAP * TILE :],
                preferred_element_type=jnp.float32,
            )
        branch_out[head, pl.ds(rows, half_rows)] = (update / totals).astype(jnp.bfloat16)

    guidance = guide_scale[0]

    def combine(head):
        swap(head).wait_recv()
        rows = pl.multiple_of(half * half_rows, half_rows)
        mine = branch_out[head, pl.ds(rows, half_rows)].astype(jnp.float32)
        other = theirs[head].astype(jnp.float32)
        cond_out = jnp.where(half == 0, mine, other)
        uncond = jnp.where(half == 0, other, mine)
        mixed[head] = (uncond + guidance * (cond_out - uncond)).astype(jnp.bfloat16)
        write(head).start()

    def step(head, carry):
        load(head, 2).wait()
        for place in places:

            @pl.when(inside(place, -1))
            def _():
                send(head, place).wait_recv()

        @pl.when(head + AHEAD < heads)
        def _():
            start_sends(head + AHEAD)

        attend(head, 1 - half)
        attend(head, half)
        swap(head).start()

        @pl.when(head > 0)
        def _():
            combine(head - 1)

        return carry

    lax.fori_loop(0, heads, step, 0)
    combine(heads - 1)

    def finish(head, carry):
        for place in places:

            @pl.when(inside(place, 1))
            def _():
                send(head, place).wait_send()

        swap(head).wait_send()
        write(head).wait()
        return carry

    lax.fori_loop(0, heads, finish, 0)


def body(query_rows, key_rows, value_rows, select, counts, guide_scale):
    tokens, width = query_rows.shape
    heads = width // HEAD_DIM
    tiles_dev = tokens // TILE
    half_rows = tokens // 2
    places = len(OFFSETS)
    pool_tiles = tiles_dev + places * CAP
    kind = query_rows.dtype
    hbm = pl.BlockSpec(memory_space=pl.ANY)
    smem = pl.BlockSpec(memory_space=pltpu.SMEM)
    sent = (heads, places, 2 * CAP * TILE, HEAD_DIM)
    return pl.pallas_call(
        kernel,
        out_shape=jax.ShapeDtypeStruct((half_rows, width), kind),
        in_specs=[hbm, hbm, hbm, smem, smem, smem],
        out_specs=hbm,
        scratch_shapes=[
            pltpu.VMEM((heads, tokens, HEAD_DIM), kind),
            pltpu.VMEM((heads, 2, tokens, HEAD_DIM), kind),
            pltpu.VMEM(sent, kind),
            pltpu.VMEM(sent, kind),
            pltpu.VMEM((heads, tokens, HEAD_DIM), kind),
            pltpu.VMEM((heads, half_rows, HEAD_DIM), kind),
            pltpu.VMEM((heads, half_rows, HEAD_DIM), kind),
            pltpu.SMEM((tiles_dev * pool_tiles,), jnp.float32),
            pltpu.SMEM((places * CAP,), jnp.int32),
            pltpu.SemaphoreType.DMA((heads, 3)),
            pltpu.SemaphoreType.DMA((heads, places)),
            pltpu.SemaphoreType.DMA((heads, places)),
            pltpu.SemaphoreType.DMA((heads,)),
            pltpu.SemaphoreType.DMA((heads,)),
            pltpu.SemaphoreType.DMA((heads,)),
        ],
        compiler_params=pltpu.CompilerParams(
            collective_id=0, has_side_effects=True, vmem_limit_bytes=62 * 1024 * 1024
        ),
        name="sparse_attention",
    )(query_rows, key_rows, value_rows, select.T, counts, guide_scale)


def solution(mesh):
    rows = P(("groups", "seq"), None)
    in_specs = (rows, rows, rows, P("groups", None), P("groups"), P("groups"))
    return jax.shard_map(body, mesh=mesh, in_specs=in_specs, out_specs=rows, check_vma=False)
```

time: 522 us -> 126 us (0.24)
  the two profiles are of different devices: /device:TPU:549 before, /device:TPU:667 now
where the time goes in v1:
time: 126 us
  Pallas kernels  123 us (98%)
  local copies, waits for them, and re-layouts  2.06 us (2%)
    pallas_call x1, Pallas kernels, body(): pl.pallas_call(kernel, out_shape=jax.ShapeDtypeStruct((half_rows, width),...  123 us

profile of v1, /device:TPU:667, one launch (start us, length us, event | category | flops | bytes accessed | tf_op | source)
XLA Modules:
  0.0 125.8 jit_solution(5440918849090255233)
XLA Ops:
  0.7 123.1 %sparse_attention.1 = bf16[256,1536]{1,0:T(8,128)(2,1)} custom-call(bf16[512,1536]{1,0:T(8,128)(2,1)} %query_hbm.1, bf16[512,1536]{1,0:T(8,128)(2,1)} %key_hbm.1, bf16[512,1536]{1,0:T(8,128)(2,1)} %value_hbm.1, s32[6,256]{1,0:T(8,128)} %bitcast.1, s32[256]{0:T(256)} %counts.1, f32[1]{0:T(128)S(6)} %copy.8.guide_scale), custom_call_target="tpu_custom_call" | custom-call | tf_op jit(solution)/shard_map/sparse_attention/pallas_call | solution.py:322
  123.8 2.1 %copy.9 = bf16[256,1536]{1,0:T(8,128)(2,1)} copy(bf16[256,1536]{1,0:T(8,128)(2,1)} %sparse_attention.1) | data formatting | bytes 1572864

commit v2 on v1

--- a/solution.py
+++ b/solution.py
@@ -23,17 +23,18 @@
     query_hbm,
     key_hbm,
     value_hbm,
-    select,
-    counts,
+    select_hbm,
+    counts_hbm,
     guide_scale,
-    out_hbm,
+    out,
     queries,
     own,
     staged,
     pool,
     branch_out,
     theirs,
-    mixed,
+    select,
+    counts,
     bias,
     send_bits,
     load_sem,
@@ -41,7 +42,7 @@
     recv_sem,
     swap_send_sem,
     swap_recv_sem,
-    out_sem,
+    table_sem,
 ):
     heads, tokens, _ = queries.shape
     tiles_dev = tokens // TILE
@@ -90,18 +91,6 @@
             device_id_type=MESH,
         )
 
-    def write(head):
-        return pltpu.make_async_copy(
-            mixed.at[head], out_hbm.at[:, columns(head)], out_sem.at[head]
-        )
-
-    def start_loads(head, carry):
-        for which in range(3):
-            load(head, which).start()
-        return carry
-
-    lax.fori_loop(0, heads, start_loads, 0)
-
     barrier = pltpu.get_barrier_semaphore()
     pl.semaphore_signal(barrier, inc=1, device_id={"seq": partner}, device_id_type=MESH)
     greeted = jnp.int32(1)
@@ -117,6 +106,29 @@
                 device_id={"seq": me + 2 * OFFSETS[place]},
                 device_id_type=MESH,
             )
+
+    tables = [
+        pltpu.make_async_copy(source, target, table_sem.at[at])
+        for at, (source, target) in enumerate(((select_hbm, select), (counts_hbm, counts)))
+    ]
+    for table in tables:
+        table.start()
+    for which in range(2):
+        load(0, which).start()
+
+    def start_loads(head, carry):
+        for which in range(2):
+            load(head, which).start()
+        return carry
+
+    def start_query_loads(head, carry):
+        load(head, 2).start()
+        return carry
+
+    lax.fori_loop(1, heads, start_loads, 0)
+    lax.fori_loop(0, heads, start_query_loads, 0)
+    for table in tables:
+        table.wait()
 
     for place in places:
         asker = jnp.clip(shard + OFFSETS[place], 0, shards - 1)
@@ -130,6 +142,29 @@
         first = lowest_bit(bits)
         send_bits[2 * place] = first
         send_bits[2 * place + 1] = lowest_bit(bits ^ first)
+
+    def stage(head):
+        for which in range(2):
+            load(head, which).wait()
+        for which in range(2):
+            tiles = [own[head, which, tile * TILE : (tile + 1) * TILE] for tile in range(tiles_dev)]
+            for place in places:
+                for slot in range(CAP):
+                    bit = send_bits[2 * place + slot]
+                    chosen = tiles[-1]
+                    for tile in range(tiles_dev - 1):
+                        chosen = jnp.where(bit == 1 << tile, tiles[tile], chosen)
+                    row = (which * CAP + slot) * TILE
+                    staged[head, place, row : row + TILE] = chosen
+
+    def start_sends(head):
+        for place in places:
+
+            @pl.when(inside(place, 1))
+            def _():
+                send(head, place).start()
+
+    stage(0)
 
     first_tile = (shard - REACH) * tiles_dev
     row_bits = []
@@ -156,6 +191,9 @@
                 (row_bits[row] & bit) != 0, jnp.float32(0), jnp.float32(-jnp.inf)
             )
 
+    pl.semaphore_wait(barrier, greeted)
+    start_sends(0)
+
     for place in places:
 
         @pl.when(jnp.logical_not(inside(place, -1)))
@@ -166,36 +204,12 @@
 
             lax.fori_loop(0, heads, clear, 0)
 
-    def stage(head):
-        for which in range(2):
-            load(head, which).wait()
-        for which in range(2):
-            tiles = [own[head, which, tile * TILE : (tile + 1) * TILE] for tile in range(tiles_dev)]
-            for place in places:
-                for slot in range(CAP):
-                    bit = send_bits[2 * place + slot]
-                    chosen = tiles[-1]
-                    for tile in range(tiles_dev - 1):
-                        chosen = jnp.where(bit == 1 << tile, tiles[tile], chosen)
-                    row = (which * CAP + slot) * TILE
-                    staged[head, place, row : row + TILE] = chosen
-
-    def start_sends(head):
-        for place in places:
-
-            @pl.when(inside(place, 1))
-            def _():
-                send(head, place).start()
-
-    stage(0)
-    pl.semaphore_wait(barrier, greeted)
-
     def fill(head, carry):
         stage(head)
 
-        @pl.when(head <= AHEAD)
-        def _():
-            start_sends(head - 1)
+        @pl.when(head < AHEAD)
+        def _():
+            start_sends(head)
 
         return carry
 
@@ -266,8 +280,8 @@
         other = theirs[head].astype(jnp.float32)
         cond_out = jnp.where(half == 0, mine, other)
         uncond = jnp.where(half == 0, other, mine)
-        mixed[head] = (uncond + guidance * (cond_out - uncond)).astype(jnp.bfloat16)
-        write(head).start()
+        mixed = uncond + guidance * (cond_out - uncond)
+        out[:, columns(head)] = mixed.astype(out.dtype)
 
     def step(head, carry):
         load(head, 2).wait()
@@ -282,8 +296,8 @@
             start_sends(head + AHEAD)
 
         attend(head, 1 - half)
+        swap(head).start()
         attend(head, half)
-        swap(head).start()
 
         @pl.when(head > 0)
         def _():
@@ -302,7 +316,6 @@
                 send(head, place).wait_send()
 
         swap(head).wait_send()
-        write(head).wait()
         return carry
 
     lax.fori_loop(0, heads, finish, 0)
@@ -316,14 +329,17 @@
     places = len(OFFSETS)
     pool_tiles = tiles_dev + places * CAP
     kind = query_rows.dtype
-    hbm = pl.BlockSpec(memory_space=pl.ANY)
-    smem = pl.BlockSpec(memory_space=pltpu.SMEM)
+    hbm = pl.BlockSpec(memory_space=pltpu.HBM)
     sent = (heads, places, 2 * CAP * TILE, HEAD_DIM)
+    operands = [
+        pltpu.with_memory_space_constraint(operand, pltpu.HBM)
+        for operand in (query_rows, key_rows, value_rows, select.T, counts)
+    ]
     return pl.pallas_call(
         kernel,
-        out_shape=jax.ShapeDtypeStruct((half_rows, width), kind),
-        in_specs=[hbm, hbm, hbm, smem, smem, smem],
-        out_specs=hbm,
+        out_shape=pltpu.VMEM((half_rows, width), kind),
+        in_specs=[hbm] * 5 + [pl.BlockSpec(memory_space=pltpu.SMEM)],
+        out_specs=pl.BlockSpec(memory_space=pltpu.VMEM),
         scratch_shapes=[
             pltpu.VMEM((heads, tokens, HEAD_DIM), kind),
             pltpu.VMEM((heads, 2, tokens, HEAD_DIM), kind),
@@ -331,7 +347,8 @@
             pltpu.VMEM(sent, kind),
             pltpu.VMEM((heads, tokens, HEAD_DIM), kind),
             pltpu.VMEM((heads, half_rows, HEAD_DIM), kind),
-            pltpu.VMEM((heads, half_rows, HEAD_DIM), kind),
+            pltpu.SMEM(select.shape[::-1], select.dtype),
+            pltpu.SMEM(counts.shape, counts.dtype),
             pltpu.SMEM((tiles_dev * pool_tiles,), jnp.float32),
             pltpu.SMEM((places * CAP,), jnp.int32),
             pltpu.SemaphoreType.DMA((heads, 3)),
@@ -339,13 +356,13 @@
             pltpu.SemaphoreType.DMA((heads, places)),
             pltpu.SemaphoreType.DMA((heads,)),
             pltpu.SemaphoreType.DMA((heads,)),
-            pltpu.SemaphoreType.DMA((heads,)),
+            pltpu.SemaphoreType.DMA((2,)),
         ],
         compiler_params=pltpu.CompilerParams(
-            collective_id=0, has_side_effects=True, vmem_limit_bytes=62 * 1024 * 1024
+            collective_id=0, has_side_effects=True, vmem_limit_bytes=48 * 1024 * 1024
         ),
         name="sparse_attention",
-    )(query_rows, key_rows, value_rows, select.T, counts, guide_scale)
+    )(*operands, guide_scale)
 
 
 def solution(mesh):

time: 126 us -> 122 us (0.968)
  Pallas kernels: 123 us -> 120 us
    pallas_call x1, Pallas kernels: 123 us -> 120 us  [body(): pl.pallas_call(kernel, out_shape=pltpu.VMEM((half_rows, width), kind), in...]
where the time goes in v2:
time: 122 us; the launch traced here: 121 us
  Pallas kernels  120 us (98%)
    pallas_call x1, Pallas kernels, body(): pl.pallas_call(kernel, out_shape=pltpu.VMEM((half_rows, width), kind), in...  120 us

profile of v2, /device:TPU:667, one launch (start us, length us, event | category | flops | bytes accessed | tf_op | source)
XLA Modules:
  0.0 121.2 jit_solution(17155686040274100431)
XLA Ops:
  0.7 119.7 %sparse_attention.1 = bf16[256,1536]{1,0:T(8,128)(2,1)S(1)} custom-call(bf16[512,1536]{1,0:T(8,128)(2,1)} %query_hbm.1, bf16[512,1536]{1,0:T(8,128)(2,1)} %key_hbm.1, bf16[512,1536]{1,0:T(8,128)(2,1)} %value_hbm.1, s32[6,256]{1,0:T(8,128)} %bitcast.1, s32[256]{0:T(256)} %counts_hbm.1, f32[1]{0:T(128)S(6)} %copy.9.guide_scale), custom_call_target="tpu_custom_call" | custom-call | tf_op jit(solution)/shard_map/sparse_attention/pallas_call | solution.py:338
  120.4 0.9 copy.8

commit v3 on v2

--- a/solution.py
+++ b/solution.py
@@ -1,3 +1,5 @@
+import functools
+
 import jax
 import jax.numpy as jnp
 from jax import lax
@@ -10,7 +12,7 @@
 REACH = 2
 CAP = 2
 OFFSETS = (-2, 2, -1, 1)
-AHEAD = 3
+LAG = 2
 LOG2E = 1.4426950408889634
 MESH = pl.DeviceIdType.MESH
 
@@ -20,6 +22,7 @@
 
 
 def kernel(
+    row_shards,
     query_hbm,
     key_hbm,
     value_hbm,
@@ -43,6 +46,7 @@
     swap_send_sem,
     swap_recv_sem,
     table_sem,
+    ready,
 ):
     heads, tokens, _ = queries.shape
     tiles_dev = tokens // TILE
@@ -55,10 +59,18 @@
     half = me % 2
     partner = me + 1 - 2 * half
     places = range(len(OFFSETS))
+    spot = shard % row_shards
 
     def inside(place, sign):
         other = shard + sign * OFFSETS[place]
         return (other >= 0) & (other < shards)
+
+    def crosses(place):
+        ahead = spot + OFFSETS[place]
+        return ahead >= row_shards if OFFSETS[place] > 0 else ahead < 0
+
+    def earlier(place):
+        return crosses(place) if OFFSETS[place] > 0 else jnp.logical_not(crosses(place))
 
     def columns(head):
         return pl.ds(pl.multiple_of(head * HEAD_DIM, HEAD_DIM), HEAD_DIM)
@@ -92,20 +104,19 @@
         )
 
     barrier = pltpu.get_barrier_semaphore()
-    pl.semaphore_signal(barrier, inc=1, device_id={"seq": partner}, device_id_type=MESH)
-    greeted = jnp.int32(1)
+
+    def greet(shift):
+        pl.semaphore_signal(barrier, inc=1, device_id={"seq": me + shift}, device_id_type=MESH)
+
+    greet(1 - 2 * half)
+    awaited = jnp.int32(1)
     for place in places:
         there = inside(place, 1)
-        greeted += there.astype(jnp.int32)
-
-        @pl.when(there)
+        awaited += (there & earlier(place)).astype(jnp.int32)
+
+        @pl.when(there & jnp.logical_not(earlier(place)))
         def _():
-            pl.semaphore_signal(
-                barrier,
-                inc=1,
-                device_id={"seq": me + 2 * OFFSETS[place]},
-                device_id_type=MESH,
-            )
+            greet(2 * OFFSETS[place])
 
     tables = [
         pltpu.make_async_copy(source, target, table_sem.at[at])
@@ -157,14 +168,31 @@
                     row = (which * CAP + slot) * TILE
                     staged[head, place, row : row + TILE] = chosen
 
-    def start_sends(head):
+    def start_early(head):
         for place in places:
-
-            @pl.when(inside(place, 1))
+            there = inside(place, 1) & earlier(place)
+            behind = crosses(place) if OFFSETS[place] == REACH else jnp.bool_(False)
+            at = jnp.where(behind & (spot == row_shards - 1), head - LAG, head)
+
+            @pl.when(there & (at >= 0) & (at < heads))
             def _():
-                send(head, place).start()
+                send(at, place).start()
 
     stage(0)
+
+    pl.semaphore_wait(barrier, awaited)
+    for place in places:
+
+        @pl.when(inside(place, 1) & earlier(place))
+        def _():
+            pl.semaphore_signal(
+                ready.at[OFFSETS.index(-OFFSETS[place])],
+                inc=1,
+                device_id={"seq": me + 2 * OFFSETS[place]},
+                device_id_type=MESH,
+            )
+
+    start_early(0)
 
     first_tile = (shard - REACH) * tiles_dev
     row_bits = []
@@ -191,8 +219,6 @@
                 (row_bits[row] & bit) != 0, jnp.float32(0), jnp.float32(-jnp.inf)
             )
 
-    pl.semaphore_wait(barrier, greeted)
-    start_sends(0)
 
     for place in places:
 
@@ -206,14 +232,32 @@
 
     def fill(head, carry):
         stage(head)
-
-        @pl.when(head < AHEAD)
-        def _():
-            start_sends(head)
-
+        start_early(head)
         return carry
 
     lax.fori_loop(1, heads, fill, 0)
+    for extra in range(LAG):
+        start_early(heads + extra)
+
+    for ahead in (True, False):
+        some = [place for place in places if (OFFSETS[place] > 0) == ahead]
+        later = [inside(place, 1) & jnp.logical_not(earlier(place)) for place in some]
+        for place, there in zip(some, later):
+
+            @pl.when(there)
+            def _():
+                pl.semaphore_wait(ready.at[place], 1)
+
+        def start_later(head, carry):
+            for place, there in zip(some, later):
+
+                @pl.when(there)
+                def _():
+                    send(head, place).start()
+
+            return carry
+
+        lax.fori_loop(0, heads, start_later, 0)
 
     factor = HEAD_DIM ** (-0.5) * LOG2E
     across = (((1,), (1,)), ((), ()))
@@ -291,10 +335,6 @@
             def _():
                 send(head, place).wait_recv()
 
-        @pl.when(head + AHEAD < heads)
-        def _():
-            start_sends(head + AHEAD)
-
         attend(head, 1 - half)
         swap(head).start()
         attend(head, half)
@@ -306,7 +346,6 @@
         return carry
 
     lax.fori_loop(0, heads, step, 0)
-    combine(heads - 1)
 
     def finish(head, carry):
         for place in places:
@@ -315,13 +354,19 @@
             def _():
                 send(head, place).wait_send()
 
+        return carry
+
+    lax.fori_loop(0, heads, finish, 0)
+    combine(heads - 1)
+
+    def finish_swap(head, carry):
         swap(head).wait_send()
         return carry
 
-    lax.fori_loop(0, heads, finish, 0)
-
-
-def body(query_rows, key_rows, value_rows, select, counts, guide_scale):
+    lax.fori_loop(0, heads, finish_swap, 0)
+
+
+def body(row_shards, query_rows, key_rows, value_rows, select, counts, guide_scale):
     tokens, width = query_rows.shape
     heads = width // HEAD_DIM
     tiles_dev = tokens // TILE
@@ -336,7 +381,7 @@
         for operand in (query_rows, key_rows, value_rows, select.T, counts)
     ]
     return pl.pallas_call(
-        kernel,
+        functools.partial(kernel, row_shards),
         out_shape=pltpu.VMEM((half_rows, width), kind),
         in_specs=[hbm] * 5 + [pl.BlockSpec(memory_space=pltpu.SMEM)],
         out_specs=pl.BlockSpec(memory_space=pltpu.VMEM),
@@ -357,6 +402,7 @@
             pltpu.SemaphoreType.DMA((heads,)),
             pltpu.SemaphoreType.DMA((heads,)),
             pltpu.SemaphoreType.DMA((2,)),
+            pltpu.SemaphoreType.REGULAR((places,)),
         ],
         compiler_params=pltpu.CompilerParams(
             collective_id=0, has_side_effects=True, vmem_limit_bytes=48 * 1024 * 1024
@@ -367,5 +413,7 @@
 
 def solution(mesh):
     rows = P(("groups", "seq"), None)
+    row_shards = len({device.coords[1] for device in mesh.devices.flat})
+    local = functools.partial(body, row_shards)
     in_specs = (rows, rows, rows, P("groups", None), P("groups"), P("groups"))
-    return jax.shard_map(body, mesh=mesh, in_specs=in_specs, out_specs=rows, check_vma=False)
+    return jax.shard_map(local, mesh=mesh, in_specs=in_specs, out_specs=rows, check_vma=False)

time: 122 us -> 120 us (0.984)
  Pallas kernels: 120 us -> 118 us
    pallas_call x1, Pallas kernels: 120 us -> 118 us  [body(): pl.pallas_call(functools.partial(kernel, row_shards), out_shape=pltpu.VME...]
where the time goes in v3:
time: 120 us
  Pallas kernels  118 us (98%)
    pallas_call x1, Pallas kernels, body(): pl.pallas_call(functools.partial(kernel, row_shards), out_shape=pltpu.VME...  118 us

profile of v3, /device:TPU:667, one launch (start us, length us, event | category | flops | bytes accessed | tf_op | source)
XLA Modules:
  0.0 120.0 jit_solution(12651497777068308928)
XLA Ops:
  0.7 118.4 %sparse_attention.1 = bf16[256,1536]{1,0:T(8,128)(2,1)S(1)} custom-call(bf16[512,1536]{1,0:T(8,128)(2,1)} %query_hbm.1, bf16[512,1536]{1,0:T(8,128)(2,1)} %key_hbm.1, bf16[512,1536]{1,0:T(8,128)(2,1)} %value_hbm.1, s32[6,256]{1,0:T(8,128)} %bitcast.1, s32[256]{0:T(256)} %counts_hbm.1, f32[1]{0:T(128)S(6)} %copy.9.guide_scale), custom_call_target="tpu_custom_call" | custom-call | tf_op jit(solution)/shard_map/sparse_attention/pallas_call | solution.py:383
  119.1 0.9 copy.8

commit v4 on v3

--- a/solution.py
+++ b/solution.py
@@ -11,8 +11,8 @@
 TILE = 128
 REACH = 2
 CAP = 2
-OFFSETS = (-2, 2, -1, 1)
-LAG = 2
+OFFSETS = (-2, -1, 2, 1)
+LAG = 1
 LOG2E = 1.4426950408889634
 MESH = pl.DeviceIdType.MESH
 
@@ -103,21 +103,6 @@
             device_id_type=MESH,
         )
 
-    barrier = pltpu.get_barrier_semaphore()
-
-    def greet(shift):
-        pl.semaphore_signal(barrier, inc=1, device_id={"seq": me + shift}, device_id_type=MESH)
-
-    greet(1 - 2 * half)
-    awaited = jnp.int32(1)
-    for place in places:
-        there = inside(place, 1)
-        awaited += (there & earlier(place)).astype(jnp.int32)
-
-        @pl.when(there & jnp.logical_not(earlier(place)))
-        def _():
-            greet(2 * OFFSETS[place])
-
     tables = [
         pltpu.make_async_copy(source, target, table_sem.at[at])
         for at, (source, target) in enumerate(((select_hbm, select), (counts_hbm, counts)))
@@ -127,6 +112,21 @@
     for which in range(2):
         load(0, which).start()
 
+    barrier = pltpu.get_barrier_semaphore()
+
+    def greet(shift):
+        pl.semaphore_signal(barrier, inc=1, device_id={"seq": me + shift}, device_id_type=MESH)
+
+    greet(1 - 2 * half)
+    awaited = jnp.int32(1)
+    for place in places:
+        there = inside(place, 1)
+        awaited += (there & earlier(place)).astype(jnp.int32)
+
+        @pl.when(there & jnp.logical_not(earlier(place)))
+        def _():
+            greet(2 * OFFSETS[place])
+
     def start_loads(head, carry):
         for which in range(2):
             load(head, which).start()
@@ -138,48 +138,6 @@
 
     lax.fori_loop(1, heads, start_loads, 0)
     lax.fori_loop(0, heads, start_query_loads, 0)
-    for table in tables:
-        table.wait()
-
-    for place in places:
-        asker = jnp.clip(shard + OFFSETS[place], 0, shards - 1)
-        bits = jnp.int32(0)
-        for row in range(tiles_dev):
-            live = counts[asker * tiles_dev + row]
-            for pick in range(picks):
-                tile = select[pick, asker * tiles_dev + row] - shard * tiles_dev
-                wanted = (pick < live) & (tile >= 0) & (tile < tiles_dev)
-                bits |= jnp.where(wanted, 1 << (tile & (tiles_dev - 1)), 0)
-        first = lowest_bit(bits)
-        send_bits[2 * place] = first
-        send_bits[2 * place + 1] = lowest_bit(bits ^ first)
-
-    def stage(head):
-        for which in range(2):
-            load(head, which).wait()
-        for which in range(2):
-            tiles = [own[head, which, tile * TILE : (tile + 1) * TILE] for tile in range(tiles_dev)]
-            for place in places:
-                for slot in range(CAP):
-                    bit = send_bits[2 * place + slot]
-                    chosen = tiles[-1]
-                    for tile in range(tiles_dev - 1):
-                        chosen = jnp.where(bit == 1 << tile, tiles[tile], chosen)
-                    row = (which * CAP + slot) * TILE
-                    staged[head, place, row : row + TILE] = chosen
-
-    def start_early(head):
-        for place in places:
-            there = inside(place, 1) & earlier(place)
-            behind = crosses(place) if OFFSETS[place] == REACH else jnp.bool_(False)
-            at = jnp.where(behind & (spot == row_shards - 1), head - LAG, head)
-
-            @pl.when(there & (at >= 0) & (at < heads))
-            def _():
-                send(at, place).start()
-
-    stage(0)
-
     pl.semaphore_wait(barrier, awaited)
     for place in places:
 
@@ -192,7 +150,54 @@
                 device_id_type=MESH,
             )
 
-    start_early(0)
+    for table in tables:
+        table.wait()
+
+    def find_wanted(place):
+        asker = jnp.clip(shard + OFFSETS[place], 0, shards - 1)
+        bits = jnp.int32(0)
+        for row in range(tiles_dev):
+            live = counts[asker * tiles_dev + row]
+            for pick in range(picks):
+                tile = select[pick, asker * tiles_dev + row]
+                wanted = (pick < live) & (tile // tiles_dev == shard)
+                bits |= jnp.where(wanted, 1 << tile % tiles_dev, 0)
+        first = lowest_bit(bits)
+        send_bits[2 * place] = first
+        send_bits[2 * place + 1] = lowest_bit(bits ^ first)
+
+    def stage(head, some):
+        for which in range(2):
+            tiles = [own[head, which, tile * TILE : (tile + 1) * TILE] for tile in range(tiles_dev)]
+            for place in some:
+                for slot in range(CAP):
+                    bit = send_bits[2 * place + slot]
+                    chosen = tiles[-1]
+                    for tile in range(tiles_dev - 1):
+                        chosen = jnp.where(bit == 1 << tile, tiles[tile], chosen)
+                    row = (which * CAP + slot) * TILE
+                    staged[head, place, row : row + TILE] = chosen
+
+    def await_tiles(head):
+        for which in range(2):
+            load(head, which).wait()
+
+    def start_early(head, some=places):
+        for place in some:
+            there = inside(place, 1) & earlier(place)
+            behind = crosses(place) if OFFSETS[place] == REACH else jnp.bool_(False)
+            at = jnp.where(behind & (spot == row_shards - 1), head - LAG, head)
+
+            @pl.when(there & (at >= 0) & (at < heads))
+            def _():
+                send(at, place).start()
+
+    for place in reversed(places):
+        find_wanted(place)
+        if place == len(OFFSETS) - 1:
+            await_tiles(0)
+        stage(0, [place])
+        start_early(0, [place])
 
     first_tile = (shard - REACH) * tiles_dev
     row_bits = []
@@ -231,7 +236,8 @@
             lax.fori_loop(0, heads, clear, 0)
 
     def fill(head, carry):
-        stage(head)
+        await_tiles(head)
+        stage(head, places)
         start_early(head)
         return carry
 

time: 120 us -> 120 us (level)
  no operation moved by 1% of the time
where the time goes in v4:
time: 120 us
  Pallas kernels  118 us (98%)
    pallas_call x1, Pallas kernels, body(): pl.pallas_call(functools.partial(kernel, row_shards), out_shape=pltpu.VME...  118 us

profile of v4, /device:TPU:667, one launch (start us, length us, event | category | flops | bytes accessed | tf_op | source)
XLA Modules:
  0.0 119.6 jit_solution(1258142322153899865)
XLA Ops:
  0.7 118.0 %sparse_attention.1 = bf16[256,1536]{1,0:T(8,128)(2,1)S(1)} custom-call(bf16[512,1536]{1,0:T(8,128)(2,1)} %query_hbm.1, bf16[512,1536]{1,0:T(8,128)(2,1)} %key_hbm.1, bf16[512,1536]{1,0:T(8,128)(2,1)} %value_hbm.1, s32[6,256]{1,0:T(8,128)} %bitcast.1, s32[256]{0:T(256)} %counts_hbm.1, f32[1]{0:T(128)S(6)} %copy.9.guide_scale), custom_call_target="tpu_custom_call" | custom-call | tf_op jit(solution)/shard_map/sparse_attention/pallas_call | solution.py:389
  118.7 0.9 copy.8

commit v5 on v4

--- a/solution.py
+++ b/solution.py
@@ -334,6 +334,10 @@
         out[:, columns(head)] = mixed.astype(out.dtype)
 
     def step(head, carry):
+        @pl.when(head > 0)
+        def _():
+            combine(head - 1)
+
         load(head, 2).wait()
         for place in places:
 
@@ -344,10 +348,6 @@
         attend(head, 1 - half)
         swap(head).start()
         attend(head, half)
-
-        @pl.when(head > 0)
-        def _():
-            combine(head - 1)
 
         return carry
 

time: 120 us -> 120 us (level)
  no operation moved by 1% of the time
where the time goes in v5:
time: 120 us
  Pallas kernels  118 us (98%)
    pallas_call x1, Pallas kernels, body(): pl.pallas_call(functools.partial(kernel, row_shards), out_shape=pltpu.VME...  118 us

profile of v5, /device:TPU:667, one launch (start us, length us, event | category | flops | bytes accessed | tf_op | source)
XLA Modules:
  0.0 119.6 jit_solution(6538312973127682808)
XLA Ops:
  0.7 118.0 %sparse_attention.1 = bf16[256,1536]{1,0:T(8,128)(2,1)S(1)} custom-call(bf16[512,1536]{1,0:T(8,128)(2,1)} %query_hbm.1, bf16[512,1536]{1,0:T(8,128)(2,1)} %key_hbm.1, bf16[512,1536]{1,0:T(8,128)(2,1)} %value_hbm.1, s32[6,256]{1,0:T(8,128)} %bitcast.1, s32[256]{0:T(256)} %counts_hbm.1, f32[1]{0:T(128)S(6)} %copy.9.guide_scale), custom_call_target="tpu_custom_call" | custom-call | tf_op jit(solution)/shard_map/sparse_attention/pallas_call | solution.py:389
  118.7 0.9 copy.8
